TPU v7x, 32 devices: a whole 2x2x4 slice. The times are simulated.
32 devices in a mesh: cls: 16 (over z, y, x), rep: 2 (over core).
Axes of the slice: x: 2, y: 2, z: 4, core: 2. Of those that a mesh axis runs over, the one named last changes fastest.
Arguments:
- queries: bfloat16 [2, 32, 768], P('rep', 'cls'), may hold values from -16 to 16
- positives: int32 [2, 32, 4], replicated, may hold values from -1 to 98303, as said below
- label_vectors: bfloat16 [98304, 768], P('cls'), may hold values from -80 to 80
- refresh_slot: int32 [], replicated, may hold values from 0 to 7
- features: bfloat16 [12288, 768], P(('cls', 'rep')), may hold values from -6 to 6
- encoder_weight: bfloat16 [768, 768], replicated, may hold values from -0.21875 to 0.21875
- encoder_gain: float32 [768], replicated, may hold values from 0.1 to 1.9
- free_vectors: bfloat16 [12288, 768], P(('cls', 'rep')), may hold values from -3 to 3
- targets: int32 [12288], replicated, may hold values from 0 to 12287, as said below
Outputs:
- loss: float32 [2, 32], P('rep', 'cls')
- query_grads: bfloat16 [2, 32, 768], P('rep', 'cls')
- refreshed_vectors: bfloat16 [12288, 768], P(('cls', 'rep'))
Inputs may be any that keep to these rules, and one draw needn't show every extreme that they name: `positives`: each row holds 1 to 4 label ids in its first places and -1 in the rest; ids may repeat within a row. `targets`: A permutation. Refreshed row t belongs to owner t // 768. The b-th aligned block of 384 entries names exactly 24 rows of every owner, all in the half b % 2 of that owner's 768 rows.
All inputs are finite; a program needn't handle non-finite values.
Results may differ from a plain program's by a relative error of at most 0.0048.
Values may be sent and summed in bfloat16 or wider, within the bound.
A program may use at most 128 MiB of HBM per device.

v0:
```python
import jax
import jax.numpy as jnp
from jax import lax
from jax.sharding import PartitionSpec as P

SLOTS = 8


def from_partner(value, axis, bit):
    mask = 2**bit
    pairs = [(source, source ^ mask) for source in range(lax.axis_size(axis))]
    return lax.ppermute(value, axis, pairs)


def combined_all(part, axis, combine):
    gathered = jax.tree.map(lambda a: lax.all_gather(a, axis), part)

    def take(source):
        return jax.tree.map(lambda a: lax.dynamic_index_in_dim(a, source, 0, False), gathered)

    return lax.fori_loop(
        1, lax.axis_size(axis), lambda source, state: combine(state, take(source)), take(0)
    )


def combine_stats(earlier, later):
    highest = jnp.maximum(earlier[0], later[0])
    summed = earlier[1] * jnp.exp(earlier[0] - highest) + later[1] * jnp.exp(later[0] - highest)
    return (highest, summed, earlier[2] + later[2])


def per_device(
    queries,
    positives,
    label_vectors,
    refresh_slot,
    features,
    encoder_weight,
    encoder_gain,
    free_vectors,
    targets,
):
    cls_count = lax.axis_size("cls")
    rep_count = lax.axis_size("rep")
    cls_index = lax.axis_index("cls")
    rep_index = lax.axis_index("rep")
    lab_rows = label_vectors.shape[0]
    feature_width = label_vectors.shape[1]
    slot_rows = lab_rows // SLOTS
    half_rows = slot_rows // rep_count
    per_owner = half_rows // cls_count
    query_rows = queries.shape[1]
    hidden = jnp.dot(features, encoder_weight, preferred_element_type=jnp.float32)
    normed = (
        hidden * lax.rsqrt(jnp.mean(hidden * hidden, axis=1, keepdims=True) + 1e-06) * encoder_gain
    )
    encoded = normed.astype(jnp.bfloat16)
    block_index = cls_index * rep_count + rep_index
    own_targets = lax.dynamic_slice_in_dim(targets, block_index * half_rows, half_rows)
    sending = encoded[jnp.argsort(own_targets)].reshape(cls_count, per_owner, feature_width)
    arrived = lax.all_to_all(sending, "cls", split_axis=0, concat_axis=0, tiled=True)
    by_source = lax.dynamic_index_in_dim(
        targets.reshape(cls_count, rep_count, half_rows), rep_index, 1, keepdims=False
    )
    row_offsets = by_source - (cls_index * slot_rows + rep_index * half_rows)
    kept_rows = (row_offsets >= 0) & (row_offsets < half_rows)
    row_keys = jnp.sort(jnp.where(kept_rows, row_offsets, half_rows), axis=1)[:, :per_owner]
    placed = arrived.reshape(half_rows, feature_width)[jnp.argsort(row_keys.reshape(-1))]
    refreshed = (free_vectors.astype(jnp.float32) + placed.astype(jnp.float32)).astype(jnp.bfloat16)
    partner = from_partner(refreshed, "rep", 0)
    first_half = jnp.where(rep_index == 0, refreshed, partner)
    second_half = jnp.where(rep_index == 0, partner, refreshed)
    fresh_block = jnp.concatenate([first_half, second_half], axis=0)
    current = lax.dynamic_update_slice(
        label_vectors, fresh_block, (refresh_slot * slot_rows, jnp.zeros((), jnp.int32))
    )
    own_queries = queries.reshape(query_rows, feature_width)
    usable_rows = lab_rows // rep_count
    usable = lax.dynamic_slice_in_dim(current, rep_index * usable_rows, usable_rows)
    first_label = cls_index * lab_rows + rep_index * usable_rows
    label_ids = (
        positives.reshape(rep_count, cls_count, query_rows, positives.shape[2])
        .transpose(1, 0, 2, 3)
        .reshape(-1, positives.shape[2])
    )
    logits = lax.dot_general(
        lax.all_gather(own_queries, ("cls", "rep"), axis=0, tiled=True),
        usable,
        (((1,), (1,)), ((), ())),
        preferred_element_type=jnp.float32,
    )
    own_offset = block_index * query_rows
    usable_count = usable.shape[0]
    label_offsets = label_ids - first_label
    valid_ids = label_ids >= 0
    present = valid_ids & (label_offsets >= 0) & (label_offsets < usable_count)
    picked = jnp.take_along_axis(logits, jnp.clip(label_offsets, 0, usable_count - 1), axis=1)
    positive_part = jnp.sum(jnp.where(present, picked, 0.0), axis=1)
    local_peak = jnp.max(logits, axis=1)
    local_total = jnp.sum(jnp.exp(logits - local_peak[:, None]), axis=1)
    local_stats = (local_peak, local_total, positive_part)
    paired = from_partner((local_stats[0], local_stats[1], local_stats[2]), "rep", 0)
    local_stats = combine_stats(local_stats, paired)
    maxima, exp_totals, positive_sums = combined_all(local_stats, "cls", combine_stats)
    log_total = maxima + jnp.log(exp_totals)
    id_count = jnp.sum(valid_ids.astype(jnp.float32), axis=1)
    loss_all = log_total - positive_sums / id_count
    inverse_count = 1.0 / id_count
    label_iota = jnp.arange(usable_count, dtype=jnp.int32)[None, :]
    target_mass = jnp.zeros(logits.shape, jnp.float32)
    for column in range(label_ids.shape[1]):
        matches = (label_offsets[:, column : column + 1] == label_iota) & present[
            :, column : column + 1
        ]
        target_mass = target_mass + jnp.where(matches, inverse_count[:, None], 0.0)
    coefficients = (jnp.exp(logits - log_total[:, None]) - target_mass).astype(jnp.bfloat16)
    own_grads = lax.psum_scatter(
        jnp.dot(coefficients, usable, preferred_element_type=jnp.float32),
        ("cls", "rep"),
        scatter_dimension=0,
        tiled=True,
    )
    own_loss = lax.dynamic_slice_in_dim(loss_all, own_offset, query_rows).reshape(1, query_rows)
    return (
        own_loss,
        own_grads.astype(jnp.bfloat16).reshape(1, query_rows, feature_width),
        refreshed,
    )


def solution(mesh):
    placed = (
        P("rep", "cls", None),
        P(),
        P("cls", None),
        P(),
        P(("cls", "rep"), None),
        P(),
        P(),
        P(("cls", "rep"), None),
        P(),
    )
    return jax.shard_map(
        per_device,
        mesh=mesh,
        in_specs=placed,
        out_specs=(P("rep", "cls"), P("rep", "cls", None), P(("cls", "rep"), None)),
        check_vma=False,
    )
```

profile of v0, /device:TPU:1, one launch (start us, length us, event | category | flops | bytes accessed | tf_op | source)
XLA Modules:
  0.0 224.6 jit_solution(2823289094446588695)
XLA Ops:
  7.2 8.1 %copy.77 = bf16[6144,768]{1,0:T(8,128)(2,1)} copy(bf16[6144,768]{1,0:T(8,128)(2,1)} %param.13) | data formatting | bytes 18874368
  15.3 3.8 %sort.39 = (s32[384]{0:T(512)}, s32[384]{0:T(512)S(1)}) sort(s32[384]{0:T(512)S(1)} %dynamic_slice.53, s32[384]{0:T(512)S(1)} %iota.11), dimensions={0}, to_apply=%region_1.0 | sort | flops 3456 | bytes 6144 | tf_op jit(solution)/shard_map/jit(argsort)/sort | solution.py:60
  19.1 0.7 multiply_reduce_fusion
  20.1 2.6 %gather_fusion = bf16[384,768]{1,0:T(8,128)(2,1)} fusion(bf16[384,768]{1,0:T(8,128)(2,1)S(1)} %multiply_convert_fusion, s32[1024]{0:T(1024)S(1)} %pad_clamp_fusion.1), kind=kCustom, calls=%fused_computation | custom fusion | bytes 1181184 | tf_op jit(solution)/shard_map/gather | solution.py:60
  22.7 7.5 %all-to-all-start = ((bf16[16,24,768]{2,1,0:T(8,128)(2,1)}), bf16[16,24,768]{2,1,0:T(8,128)(2,1)S(1)}, u32[]{:S(2)}, u32[]{:S(2)}) async-start(bf16[16,24,768]{2,1,0:T(8,128)(2,1)} %bitcast.3), calls=%async_computation | async-start | bytes 1179648 | tf_op jit(solution)/shard_map/all_to_all | solution.py:61
  30.4 0.6 bitcast_select_fusion
  33.0 3.3 %sort.43.cloned.1.call-done = s32[16,384]{1,0:T(8,128)} async-done(((s32[16,384]{1,0:T(8,128)}), s32[16,384]{1,0:T(8,128)}) %sort.43.cloned.1.call-update) | async-done | bytes 24592 | tf_op jit(solution)/shard_map/jit(sort)/sort | solution.py:67
  36.3 0.7 slice.48
  37.0 3.8 %sort.41 = (s32[384]{0:T(512)}, s32[384]{0:T(512)S(1)}) sort(s32[384]{0:T(512)S(1)} %reshape.113, s32[384]{0:T(512)S(1)} %iota.12), dimensions={0}, to_apply=%region_3.4 | sort | flops 3456 | bytes 6144 | tf_op jit(solution)/shard_map/jit(argsort)/sort | solution.py:68
  40.8 2.8 %all-to-all-done = bf16[16,24,768]{2,1,0:T(8,128)(2,1)S(1)} async-done(((bf16[16,24,768]{2,1,0:T(8,128)(2,1)}), bf16[16,24,768]{2,1,0:T(8,128)(2,1)S(1)}, u32[]{:S(2)}, u32[]{:S(2)}) %all-to-all-start) | async-done | bytes 589856 | tf_op jit(solution)/shard_map/all_to_all | solution.py:61
  43.6 2.2 gather_fusion.1
  46.0 3.9 %collective-permute-start = (bf16[384,768]{1,0:T(8,128)(2,1)S(1)}, bf16[384,768]{1,0:T(8,128)(2,1)S(1)}, u32[]{:S(2)}, u32[]{:S(2)}) collective-permute-start(bf16[384,768]{1,0:T(8,128)(2,1)S(1)} %add_convert_fusion), channel_id=1, source_target_pairs={{0,1},{1,0},{2,3},{3,2},{4,5},{5,4},{6,7},{7,6},{8,9},{9,8},{10,11... | collective-permute-start | bytes 1769480 | tf_op jit(solution)/shard_map/ppermute | solution.py:12
  50.4 0.6 dynamic-slice
  51.6 39.5 %all-gather = bf16[1,64,768]{2,0,1:T(2,128)(2,1)S(1)} all-gather(bf16[1,2,768]{2,0,1:T(2,128)(2,1)S(1)} %copy.38), channel_id=2, replica_groups=mesh['cls'=16,'rep'=2] {'cls','rep'}, dimensions={1}, use_global_device_ids=true | all-gather | bytes 101376 | tf_op jit(solution)/shard_map/all_gather | solution.py:87
  91.8 1.1 maximum_dynamic-update-slice_fusion
  92.9 4.0 %fusion.38 = (f32[64]{0:T(128)S(1)}, f32[3072,64]{0,1:T(8,128)S(1)}) fusion(bf16[1,64,768]{2,0,1:T(2,128)(2,1)S(1)} %all-gather, bf16[6144,768]{1,0:T(8,128)(2,1)} %maximum_dynamic-update-slice_fusion, s32[]{:T(128)S(6)} %select_n.102), kind=kOutput, calls=%fused_computation.90 | convolution fusion | flops 302186432 | bytes 5603588 | tf_op jit(solution)/shard_map/dot_general | solution.py:86
  96.9 2.4 %gather_fusion.2 = f32[256]{0:T(256)S(1)} fusion(f32[64,3072]{1,0:T(8,128)S(1)} %bitcast.69, s32[256]{0:T(256)S(1)} %reshape.133), kind=kCustom, calls=%fused_computation.2 | custom fusion | bytes 4096 | tf_op jit(solution)/shard_map/jit(take_along_axis)/gather | solution.py:97
  101.2 0.4 collective-permute-done.1
  102.1 57.8 %all-reduce.4 = (f32[1024]{0:T(1024)S(1)}, f32[1024]{0:T(1024)S(1)}, f32[1024]{0:T(1024)S(1)}) all-reduce(f32[1024]{0:T(1024)S(1)} %maximum_dynamic-update-slice_fusion.1, f32[1024]{0:T(1024)S(1)} %add_dynamic-update-slice_fusion.1, f32[1024]{0:T(1024)S(1)} %add_dynamic-update-slice_fusion), channel_id=3, replica_groups=mesh['cls'=16,'rep'=2] {'cls'}, use_global_device_ids=true, to_apply=%add | all-reduce | flops 3072 | bytes 24576
  160.1 0.7 while.19
  160.8 3.8 %fusion.7 = f32[64,768]{1,0:T(8,128)S(1)} fusion(bf16[6144,768]{1,0:T(8,128)(2,1)} %maximum_dynamic-update-slice_fusion, s32[]{:T(128)S(6)} %select_n.102, s32[64]{0:T(128)S(1)} %get-tuple-element.191, s32[64]{0:T(128)S(1)} %get-tuple-element.189, s32[64]{0:T(128)S(1)} %get-tuple-element.190, f32[64]{0:T(128)S(1)} %get-tuple-element.223, ...), kind=kOutput, calls=%fused_computation.13 | convolution fusion | flops 305528832 | bytes 5703428 | tf_op jit(solution)/shard_map/dot_general | solution.py:118
  164.6 51.9 %all-reduce.6 = bf16[64,768]{1,0:T(8,128)(2,1)S(1)} all-reduce(f32[64,768]{1,0:T(8,128)S(1)} %fusion.7), channel_id=6, replica_groups=mesh['cls'=16,'rep'=2] {'cls','rep'}, use_global_device_ids=true, to_apply=%region_10.11.clone | all-reduce | flops 49152 | bytes 294912
  216.6 0.6 fusion.32
  217.1 0.6 dynamic-slice_bitcast_fusion
  (96 shorter events, 6.0 us)
Async XLA Ops:
  7.2 12.0 %copy-start = (bf16[768,768]{1,0:T(8,128)(2,1)S(1)}, bf16[768,768]{1,0:T(8,128)(2,1)}, u32[]{:S(2)}) copy-start(bf16[768,768]{1,0:T(8,128)(2,1)} %param.16) | copy-start | bytes 3538948
  7.2 11.9 %copy-start.2 = (bf16[384,768]{1,0:T(8,128)(2,1)S(1)}, bf16[384,768]{1,0:T(8,128)(2,1)}, u32[]{:S(2)}) copy-start(bf16[384,768]{1,0:T(8,128)(2,1)} %param.15) | copy-start | bytes 1769476
  7.2 8.1 %copy-start.4 = (s32[12288]{0:T(1024)S(1)}, s32[12288]{0:T(1024)}, u32[]{:S(2)}) copy-start(s32[12288]{0:T(1024)} %param.19) | copy-start | bytes 147460
  19.1 0.7 copy-start.5
  22.7 8.3 %copy-start.6 = (s32[2,32,4]{1,2,0:T(4,128)S(1)}, s32[2,32,4]{1,2,0:T(4,128)}, u32[]{:S(2)}) copy-start(s32[2,32,4]{1,2,0:T(4,128)} %param.12) | copy-start | bytes 3076
  22.7 9.9 %copy-start.7 = (bf16[1,2,768]{2,1,0:T(2,128)(2,1)S(1)}, bf16[1,2,768]{2,1,0:T(2,128)(2,1)}, u32[]{:S(2)}) copy-start(bf16[1,2,768]{2,1,0:T(2,128)(2,1)} %param.11) | copy-start | bytes 9220
  22.7 20.9 %all-to-all-start = ((bf16[16,24,768]{2,1,0:T(8,128)(2,1)}), bf16[16,24,768]{2,1,0:T(8,128)(2,1)S(1)}, u32[]{:S(2)}, u32[]{:S(2)}) async-start(bf16[16,24,768]{2,1,0:T(8,128)(2,1)} %bitcast.3), calls=%async_computation | async-start | bytes 1179648 | tf_op jit(solution)/shard_map/all_to_all | solution.py:61
  30.2 6.0 %sort.43.cloned.1.call-start = ((), (), s32[]{:S(2)}) async-start(), calls=%async_computation.1 | async-start | bytes 73760 | tf_op jit(solution)/shard_map/jit(sort)/sort | solution.py:67
  43.6 2.2 copy-start.3
  45.8 4.6 %copy-start.8 = (u32[32]{0:T(128)S(1)}, u32[32]{0:T(128)}, u32[]{:S(2)}) copy-start(u32[32]{0:T(128)} %constant.125) | copy-start | bytes 388
  46.0 45.8 %copy-start.1 = (bf16[384,768]{1,0:T(8,128)(2,1)}, bf16[384,768]{1,0:T(8,128)(2,1)S(1)}, u32[]{:S(2)}) copy-start(bf16[384,768]{1,0:T(8,128)(2,1)S(1)} %add_convert_fusion) | copy-start | bytes 1769476
  46.0 45.6 %collective-permute-start = (bf16[384,768]{1,0:T(8,128)(2,1)S(1)}, bf16[384,768]{1,0:T(8,128)(2,1)S(1)}, u32[]{:S(2)}, u32[]{:S(2)}) collective-permute-start(bf16[384,768]{1,0:T(8,128)(2,1)S(1)} %add_convert_fusion), channel_id=1, source_target_pairs={{0,1},{1,0},{2,3},{3,2},{4,5},{5,4},{6,7},{7,6},{8,9},{9,8},{10,11... | collective-permute-start | bytes 1769480 | tf_op jit(solution)/shard_map/ppermute | solution.py:12
  99.9 1.2 collective-permute-start.3
  100.4 1.2 collective-permute-start.1
  100.8 1.2 collective-permute-start.2
Sparse Core Ops, SparseCore 0:
  33.4 2.5 sort.45.cloned.1.call-done
  (1 shorter events, 0.0 us)
where the time goes:
time: 226 us; the launch traced here: 225 us
  blocking collectives  149 us (66%)
  local copies, waits for them, and re-layouts  24.2 us (11%)
  between operations  15.7 us (7%)
  starting transfers between devices  12.2 us (5%)
  other arithmetic  10.9 us (5%)
  matrix products  8.49 us (4%)
  waiting for transfers between devices  3.61 us (2%)
    unnamed x2, blocking collectives  110 us
    all_gather x1, blocking collectives, per_device(): lax.all_gather(own_queries, ('cls', 'rep'), axis=0, tiled=True)  39.5 us
    unnamed x25, local copies, waits for them, and re-layouts  8.71 us
    all_to_all x1, starting transfers between devices, per_device(): lax.all_to_all(sending, 'cls', split_axis=0, concat_axis=0, tiled=True)  7.53 us
    ppermute x4, starting transfers between devices, from_partner(): return lax.ppermute(value, axis, pairs)  4.66 us
  transfers between devices with their start and end apart: 5, of which 4 were waited for; matrix products, arithmetic and copies ran while one was open for 4% of the time, Pallas kernels for 0%

commit v1 on v0

v1 whole, which is shorter than its diff:
```python
import functools

import jax
import jax.numpy as jnp
from jax import lax
from jax.experimental import pallas as pl
from jax.experimental.pallas import tpu as pltpu
from jax.sharding import PartitionSpec as P

SLOTS = 8
NEG = -1e30
STATS = 128
NT = (((1,), (1,)), ((), ()))


def to_column(row, eye):
    return jnp.sum(jnp.where(eye, row, 0.0), axis=1, keepdims=True)


def step_kernel(
    n_cls,
    n_rep,
    slot_ref,
    queries_ref,
    positives_ref,
    targets_ref,
    gain_ref,
    labels_hbm,
    features_hbm,
    weight_hbm,
    free_hbm,
    loss_ref,
    grads_ref,
    refreshed_ref,
    labels,
    features,
    weight,
    free,
    q_slots,
    q_rows,
    out_rows,
    in_rows,
    staged,
    logits,
    mixed,
    half_out,
    half_in,
    shares_out,
    shares_in,
    load_sem,
    q_send,
    q_recv,
    row_send,
    row_recv,
    half_send,
    half_recv,
    share_send,
    share_recv,
):
    f32, bf16 = jnp.float32, jnp.bfloat16
    cls = lax.axis_index("cls")
    rep = lax.axis_index("rep")
    total = n_cls * n_rep
    me = cls * n_rep + rep
    half_rows, width = features.shape
    padded = out_rows.shape[1]
    per_owner = half_rows // n_cls
    query_rows = q_slots.shape[1]
    n_query = q_rows.shape[0]
    own_half = n_query // n_rep
    usable, slot_rows = labels.shape[0], half_rows * n_rep
    lab_rows = usable * n_rep

    def slot_of(c, r):
        return r * n_cls + c

    barrier = pltpu.get_barrier_semaphore()

    def greet(k, carry):
        other = lax.rem(me + k, total)
        pl.semaphore_signal(barrier, inc=1, device_id=(other // n_rep, lax.rem(other, n_rep)))
        return carry

    lax.fori_loop(1, total, greet, 0)

    loads = [
        pltpu.make_async_copy(features_hbm, features, load_sem.at[0]),
        pltpu.make_async_copy(weight_hbm, weight, load_sem.at[1]),
        pltpu.make_async_copy(free_hbm, free, load_sem.at[2]),
    ]
    chunks = usable // slot_rows
    for k in range(chunks):
        start = pl.multiple_of(rep * usable + k * slot_rows, slot_rows)
        loads.append(
            pltpu.make_async_copy(
                labels_hbm.at[pl.ds(start, slot_rows)],
                labels.at[pl.ds(k * slot_rows, slot_rows)],
                load_sem.at[3 + k],
            )
        )
    for copy in loads:
        copy.start()

    mine = slot_of(cls, rep)
    q_slots[mine] = queries_ref[0]

    row_i = lax.broadcasted_iota(jnp.int32, (half_rows, half_rows), 0)
    col_i = lax.broadcasted_iota(jnp.int32, (half_rows, half_rows), 1)
    eye = row_i == col_i
    t_row = targets_ref[me].astype(f32)
    t_col = to_column(t_row, eye)
    rank = jnp.sum(jnp.where(t_col < t_row, 1.0, 0.0), axis=0, keepdims=True)
    owner = jnp.floor((rank + 0.5) * (1.0 / per_owner))
    place = owner * padded + (rank - owner * per_owner)
    place_i = lax.broadcasted_iota(jnp.int32, (n_cls * padded, half_rows), 0)
    pick = jnp.where(place_i == place.astype(jnp.int32), 1.0, 0.0).astype(bf16)
    loads[0].wait()
    ordered = jnp.dot(pick, features[...], preferred_element_type=f32).astype(bf16)
    loads[1].wait()
    hidden = jnp.dot(ordered, weight[...], preferred_element_type=f32)
    scale = lax.rsqrt(jnp.mean(hidden * hidden, axis=1, keepdims=True) + 1e-06)
    encoded = hidden * scale * gain_ref[...]
    for c in range(n_cls):
        out_rows[c] = encoded[c * padded : (c + 1) * padded].astype(bf16)

    pl.semaphore_wait(barrier, total - 1)

    def query_copy(other, slot):
        return pltpu.make_async_remote_copy(
            src_ref=q_slots.at[mine],
            dst_ref=q_slots.at[slot],
            send_sem=q_send.at[other],
            recv_sem=q_recv.at[slot],
            device_id=(other // n_rep, lax.rem(other, n_rep)),
        )

    def row_copy(other, slot):
        return pltpu.make_async_remote_copy(
            src_ref=out_rows.at[other],
            dst_ref=in_rows.at[slot],
            send_sem=row_send.at[other],
            recv_sem=row_recv.at[slot],
            device_id=(other, rep),
        )

    def share_copy(other, slot):
        return pltpu.make_async_remote_copy(
            src_ref=shares_out.at[other],
            dst_ref=shares_in.at[slot],
            send_sem=share_send.at[other],
            recv_sem=share_recv.at[slot],
            device_id=(other, rep),
        )

    def send_query(k, carry):
        query_copy(lax.rem(me + k, total), mine).start()
        return carry

    lax.fori_loop(1, total, send_query, 0)

    def send_rows(k, carry):
        row_copy(lax.rem(cls + k, n_cls), cls).start()
        return carry

    lax.fori_loop(1, n_cls, send_rows, 0)
    in_rows[cls] = out_rows[cls]

    my_base = (cls * slot_rows + rep * half_rows).astype(f32)
    wanted = my_base + row_i.astype(f32)

    def find(c, acc):
        t_c = targets_ref[c * n_rep + rep].astype(f32)
        return acc + jnp.where(t_c == wanted, (c + 1).astype(f32), 0.0)

    found = lax.fori_loop(0, n_cls, find, jnp.zeros((half_rows, half_rows), f32))
    src_col = jnp.sum(found, axis=1, keepdims=True) - 1.0
    src_row = jnp.sum(jnp.where(eye, src_col, 0.0), axis=0, keepdims=True)
    before = jnp.where((src_col == src_row) & (col_i < row_i), 1.0, 0.0)
    seat = src_col * padded + jnp.sum(before, axis=1, keepdims=True)
    seat_i = lax.broadcasted_iota(jnp.int32, (half_rows, n_cls * padded), 1)
    seating = jnp.where(seat_i == seat.astype(jnp.int32), 1.0, 0.0).astype(bf16)

    def get_query(k, carry):
        other = lax.rem(me + k, total)
        slot = slot_of(other // n_rep, lax.rem(other, n_rep))
        query_copy(other, slot).wait_recv()
        return carry

    lax.fori_loop(1, total, get_query, 0)
    for s in range(total):
        q_rows[s * query_rows : (s + 1) * query_rows] = q_slots[s].astype(f32)
    q = q_rows[...].astype(bf16)

    ids = positives_ref[...]
    slot_start = slot_ref[0] * slot_rows
    n_pos = ids.shape[1]

    def counts_of(first, cols):
        label = first + lax.broadcasted_iota(jnp.int32, (n_query, cols), 1)
        count = jnp.zeros((n_query, cols), f32)
        for p in range(n_pos):
            count = count + jnp.where(ids[:, p : p + 1] == label, 1.0, 0.0)
        return count

    def weighted(block, peak, count, vectors):
        power = jnp.exp(block - peak)
        high = power.astype(bf16)
        low = (power - high.astype(f32)).astype(bf16)
        n = n_query
        cols = block.shape[1]
        mixed[0:n, 0:cols] = high
        mixed[n : 2 * n, 0:cols] = low
        mixed[2 * n : 3 * n, 0:cols] = count.astype(bf16)
        out = jnp.dot(mixed[:, 0:cols], vectors, preferred_element_type=f32)
        exp_sum = jnp.sum(power, axis=1, keepdims=True)
        pos_sum = jnp.sum(count * jnp.where(count > 0.0, block, 0.0), axis=1, keepdims=True)
        return out[0:n] + out[n : 2 * n], out[2 * n : 3 * n], exp_sum, pos_sum

    peak = jnp.full((n_query, 1), NEG, f32)
    for k in range(chunks):
        loads[3 + k].wait()
        at = slice(k * slot_rows, (k + 1) * slot_rows)
        block = lax.dot_general(q, labels[at], NT, preferred_element_type=f32)
        fresh = slot_start == rep * usable + k * slot_rows
        block = jnp.where(fresh, NEG, block)
        logits[:, at] = block
        peak = jnp.maximum(peak, jnp.max(block, axis=1, keepdims=True))
    grad = jnp.zeros((n_query, width), f32)
    hits = jnp.zeros((n_query, width), f32)
    exp_sum = jnp.zeros((n_query, 1), f32)
    pos_sum = jnp.zeros((n_query, 1), f32)
    for k in range(chunks):
        at = slice(k * slot_rows, (k + 1) * slot_rows)
        first = cls * lab_rows + rep * usable + k * slot_rows
        fresh = slot_start == rep * usable + k * slot_rows
        count = jnp.where(fresh, 0.0, counts_of(first, slot_rows))
        g, t, e, s = weighted(logits[:, at], peak, count, labels[at])
        grad, hits, exp_sum, pos_sum = grad + g, hits + t, exp_sum + e, pos_sum + s

    fresh_count = counts_of(cls * lab_rows + slot_start + rep * half_rows, half_rows)

    def get_rows(k, carry):
        other = lax.rem(cls + n_cls - k, n_cls)
        row_copy(other, other).wait_recv()
        return carry

    lax.fori_loop(1, n_cls, get_rows, 0)
    for c in range(n_cls):
        staged[c * padded : (c + 1) * padded] = in_rows[c].astype(f32)
    placed = jnp.dot(seating, staged[...].astype(bf16), preferred_element_type=f32)
    loads[2].wait()
    refreshed_ref[...] = (free[...].astype(f32) + placed).astype(bf16)
    vectors = refreshed_ref[...]
    block = lax.dot_general(q, vectors, NT, preferred_element_type=f32)
    fresh_peak = jnp.max(block, axis=1, keepdims=True)
    g, t, e, s = weighted(block, fresh_peak, fresh_count, vectors)
    top = jnp.maximum(peak, fresh_peak)
    a, b = jnp.exp(peak - top), jnp.exp(fresh_peak - top)
    grad, hits = grad * a + g * b, hits + t
    exp_sum, pos_sum = exp_sum * a + e * b, pos_sum + s

    lane = lax.broadcasted_iota(jnp.int32, (n_query, STATS), 1)
    stats = jnp.where(lane == 0, top, jnp.where(lane == 1, exp_sum, pos_sum))
    for r in range(n_rep):
        at = slice(r * own_half, (r + 1) * own_half)
        half_out[r, :, 0:width] = grad[at]
        half_out[r, :, width : 2 * width] = hits[at]
        half_out[r, :, 2 * width :] = stats[at]
    partner = 1 - rep
    swap = pltpu.make_async_remote_copy(
        src_ref=half_out.at[partner],
        dst_ref=half_in,
        send_sem=half_send,
        recv_sem=half_recv,
        device_id=(cls, partner),
    )
    swap.start()

    def merge(x, y):
        xs, ys = x[:, 2 * width :], y[:, 2 * width :]
        m = jnp.maximum(xs[:, 0:1], ys[:, 0:1])
        a, b = jnp.exp(xs[:, 0:1] - m), jnp.exp(ys[:, 0:1] - m)
        both = x[:, 0:width] * a + y[:, 0:width] * b
        return (
            both,
            x[:, width : 2 * width] + y[:, width : 2 * width],
            m,
            xs[:, 1:2] * a + ys[:, 1:2] * b,
            xs[:, 2:3] + ys[:, 2:3],
        )

    swap.wait_recv()
    both, hits, m, exp_sum, pos_sum = merge(half_out[rep], half_in[...])
    lane = lax.broadcasted_iota(jnp.int32, (own_half, STATS), 1)
    stats = jnp.where(lane == 0, m, jnp.where(lane == 1, exp_sum, pos_sum))
    for c in range(n_cls):
        at = slice(c * query_rows, (c + 1) * query_rows)
        shares_out[c, :, 0:width] = both[at]
        shares_out[c, :, width : 2 * width] = hits[at]
        shares_out[c, :, 2 * width :] = stats[at]

    def send_share(k, carry):
        share_copy(lax.rem(cls + k, n_cls), cls).start()
        return carry

    lax.fori_loop(1, n_cls, send_share, 0)
    shares_in[cls] = shares_out[cls]

    own_ids = positives_ref[pl.ds(mine * query_rows, query_rows), :]
    id_count = jnp.sum(jnp.where(own_ids >= 0, 1.0, 0.0), axis=1, keepdims=True)

    def get_share(k, carry):
        other = lax.rem(cls + n_cls - k, n_cls)
        share_copy(other, other).wait_recv()
        return carry

    lax.fori_loop(1, n_cls, get_share, 0)

    def peak_of(c, m):
        return jnp.maximum(m, shares_in[c, :, 2 * width : 2 * width + 1])

    m = lax.fori_loop(0, n_cls, peak_of, jnp.full((query_rows, 1), NEG, f32))

    def add(c, state):
        grad, hits, exp_sum, pos_sum = state
        share = shares_in[c]
        a = jnp.exp(share[:, 2 * width : 2 * width + 1] - m)
        return (
            grad + a * share[:, 0:width],
            hits + share[:, width : 2 * width],
            exp_sum + a * share[:, 2 * width + 1 : 2 * width + 2],
            pos_sum + share[:, 2 * width + 2 : 2 * width + 3],
        )

    zero = jnp.zeros((query_rows, 1), f32)
    wide = jnp.zeros((query_rows, width), f32)
    grad, hits, exp_sum, pos_sum = lax.fori_loop(0, n_cls, add, (wide, wide, zero, zero))
    loss = m + jnp.log(exp_sum) - pos_sum / id_count
    loss_ref[...] = jnp.broadcast_to(loss, loss_ref.shape)
    grads_ref[0] = (grad / exp_sum - hits / id_count).astype(bf16)

    def end_query(k, carry):
        query_copy(lax.rem(me + k, total), mine).wait_send()
        return carry

    lax.fori_loop(1, total, end_query, 0)

    def end_rows(k, carry):
        other = lax.rem(cls + k, n_cls)
        row_copy(other, cls).wait_send()
        share_copy(other, cls).wait_send()
        return carry

    lax.fori_loop(1, n_cls, end_rows, 0)
    swap.wait_send()


def per_device(
    n_cls,
    n_rep,
    queries,
    positives,
    label_vectors,
    refresh_slot,
    features,
    encoder_weight,
    encoder_gain,
    free_vectors,
    targets,
):
    f32, bf16 = jnp.float32, jnp.bfloat16
    total = n_cls * n_rep
    lab_rows, width = label_vectors.shape
    usable = lab_rows // n_rep
    slot_rows = lab_rows // SLOTS
    half_rows = slot_rows // n_rep
    per_owner = half_rows // n_cls
    padded = -(-per_owner // 8) * 8
    query_rows = queries.shape[1]
    n_query = total * query_rows
    share = 2 * width + STATS
    vmem = pl.BlockSpec(memory_space=pltpu.VMEM)
    smem = pl.BlockSpec(memory_space=pltpu.SMEM)
    hbm = pl.BlockSpec(memory_space=pl.ANY)
    dma = pltpu.SemaphoreType.DMA
    loss, grads, refreshed = pl.pallas_call(
        functools.partial(step_kernel, n_cls, n_rep),
        out_shape=(
            jax.ShapeDtypeStruct((query_rows, 128), f32),
            jax.ShapeDtypeStruct((1, query_rows, width), bf16),
            jax.ShapeDtypeStruct((half_rows, width), bf16),
        ),
        in_specs=[smem, vmem, vmem, vmem, vmem, hbm, hbm, hbm, hbm],
        out_specs=(vmem, vmem, vmem),
        scratch_shapes=[
            pltpu.VMEM((usable, width), bf16),
            pltpu.VMEM((half_rows, width), bf16),
            pltpu.VMEM((width, width), bf16),
            pltpu.VMEM((half_rows, width), bf16),
            pltpu.VMEM((total, query_rows, width), bf16),
            pltpu.VMEM((n_query, width), f32),
            pltpu.VMEM((n_cls, padded, width), bf16),
            pltpu.VMEM((n_cls, padded, width), bf16),
            pltpu.VMEM((n_cls * padded, width), f32),
            pltpu.VMEM((n_query, usable), f32),
            pltpu.VMEM((3 * n_query, slot_rows), bf16),
            pltpu.VMEM((n_rep, n_query // n_rep, share), f32),
            pltpu.VMEM((n_query // n_rep, share), f32),
            pltpu.VMEM((n_cls, query_rows, share), f32),
            pltpu.VMEM((n_cls, query_rows, share), f32),
            dma((3 + usable // slot_rows,)),
            dma((total,)),
            dma((total,)),
            dma((n_cls,)),
            dma((n_cls,)),
            dma,
            dma,
            dma((n_cls,)),
            dma((n_cls,)),
        ],
        compiler_params=pltpu.CompilerParams(
            collective_id=0, has_side_effects=True, vmem_limit_bytes=60 * 2**20
        ),
    )(
        refresh_slot.reshape(1),
        queries,
        positives.reshape(n_query, positives.shape[2]),
        targets.reshape(total, 1, half_rows),
        encoder_gain.reshape(1, width),
        label_vectors,
        features,
        encoder_weight,
        free_vectors,
    )
    return loss[:, 0].reshape(1, query_rows), grads, refreshed


def solution(mesh):
    placed = (
        P("rep", "cls", None),
        P(),
        P("cls", None),
        P(),
        P(("cls", "rep"), None),
        P(),
        P(),
        P(("cls", "rep"), None),
        P(),
    )
    return jax.shard_map(
        functools.partial(per_device, mesh.shape["cls"], mesh.shape["rep"]),
        mesh=mesh,
        in_specs=placed,
        out_specs=(P("rep", "cls"), P("rep", "cls", None), P(("cls", "rep"), None)),
        check_vma=False,
    )
```

time: 226 us -> 44.7 us (0.20)
  blocking collectives: 149 us -> 0 us
  Pallas kernels: 0 us -> 36 us
  local copies, waits for them, and re-layouts: 24.2 us -> 7.13 us
  between operations: 15.7 us -> 1.29 us
  starting transfers between devices: 12.2 us -> 0 us
  other arithmetic: 10.9 us -> 0 us
  matrix products: 8.49 us -> 0 us
  waiting for transfers between devices: 3.61 us -> 0 us
    unnamed x2 -> x0, blocking collectives: 110 us -> none
    all_gather x1 -> x0, blocking collectives: 39.5 us -> none  [per_device(): lax.all_gather(own_queries, ('cls', 'rep'), axis=0, tiled=True)]
    pallas_call x0 -> x1, Pallas kernels: none -> 36 us  [per_device(): pl.pallas_call(functools.partial(step_kernel, n_cls, n_rep), out_shape=(j...]
    dot_general x3 -> x0, matrix products: 8.49 us -> none  [the longest x1 3.97 us: per_device(): lax.dot_general(lax.all_gather(own_queries, ('cls', 'rep'), axis=0, tiled...]
    gather x6 -> x0, local copies, waits for them, and re-layouts: 7.7 us -> none  [the longest x4 2.9 us: per_device(): jnp.take_along_axis(logits, jnp.clip(label_offsets, 0, usable_count - 1),...]
    sort x2 -> x0, other arithmetic: 7.54 us -> none  [the longest x1 3.77 us: per_device(): jnp.argsort(own_targets)]
    all_to_all x1 -> x0, starting transfers between devices: 7.53 us -> none  [per_device(): lax.all_to_all(sending, 'cls', split_axis=0, concat_axis=0, tiled=True)]
    ppermute x4 -> x0, starting transfers between devices: 4.66 us -> none  [from_partner(): return lax.ppermute(value, axis, pairs)]
  transfers between devices with their start and end apart: 5 -> 0, of which waited for: 4 -> 0; matrix products, arithmetic and copies ran while one was open for 4% -> 0% of each run, Pallas kernels for 0% -> 0%
where the time goes in v1:
time: 44.7 us; the launch traced here: 44.4 us
  Pallas kernels  36 us (81%)
  local copies, waits for them, and re-layouts  7.13 us (16%)
  between operations  1.29 us (3%)
    pallas_call x1, Pallas kernels, per_device(): pl.pallas_call(functools.partial(step_kernel, n_cls, n_rep), out_shape=(j...  36 us
    unnamed x3, local copies, waits for them, and re-layouts  4.57 us
    slice x1, local copies, waits for them, and re-layouts, per_device(): return (loss[:, 0].reshape(1, query_rows), grads, refreshed)  1.29 us
    reshape x1, local copies, waits for them, and re-layouts, per_device(): encoder_gain.reshape(1, width)  1.27 us

profile of v1, /device:TPU:1, one launch (start us, length us, event | category | flops | bytes accessed | tf_op | source)
XLA Modules:
  0.0 44.4 jit_solution(15349589662972078504)
XLA Ops:
  1.3 1.3 %reshape.21.gain_ref = f32[1,768]{1,0:T(1,128)} reshape(f32[768]{0:T(1024)} %param.15) | data formatting | bytes 6144 | tf_op jit(solution)/shard_map/reshape | solution.py:429
  2.5 1.4 %copy.13 = s32[2,32,4]{2,1,0:T(8,128)} copy(s32[2,32,4]{1,2,0:T(4,128)} %param.10) | data formatting | bytes 2048 | tf_op args[1]
  3.9 36.0 %shard_map.112 = (f32[2,128]{1,0:T(2,128)}, bf16[1,2,768]{2,1,0:T(2,128)(2,1)}, bf16[384,768]{1,0:T(8,128)(2,1)}) custom-call(s32[1]{0:T(128)} %bitcast.4.slot_ref, bf16[1,2,768]{2,1,0:T(2,128)(2,1)} %queries_ref.1, s32[64,4]{1,0:T(8,128)} %bitcast.5, s32[32,1,384]{2,1,0:T(1,128)} %bitcast.6, f32[1,768]{1,0:T(1,128)} %reshape.21.gain_ref, ...), custom_call_target="tpu_custom_call" | custom-call | tf_op jit(solution)/shard_map/pallas_call | solution.py:386
  39.9 1.3 %slice_reduce_fusion = f32[2]{0:T(128)} fusion(f32[2,128]{1,0:T(2,128)} %get-tuple-element.6), kind=kLoop, calls=%fused_computation | loop fusion | bytes 16 | tf_op jit(solution)/shard_map/slice | solution.py:435
  41.2 1.3 %copy.17 = bf16[1,2,768]{2,1,0:T(2,128)(2,1)} copy(bf16[1,2,768]{2,1,0:T(2,128)(2,1)} %get-tuple-element.13) | data formatting | bytes 6144
  42.4 1.9 %copy.18 = bf16[384,768]{1,0:T(8,128)(2,1)} copy(bf16[384,768]{1,0:T(8,128)(2,1)} %get-tuple-element.14) | data formatting | bytes 1179648

commit v2 on v1

--- a/solution.py
+++ b/solution.py
@@ -15,6 +15,11 @@
 
 def to_column(row, eye):
     return jnp.sum(jnp.where(eye, row, 0.0), axis=1, keepdims=True)
+
+
+def eye_of(n):
+    shape = (n, n)
+    return lax.broadcasted_iota(jnp.int32, shape, 0) == lax.broadcasted_iota(jnp.int32, shape, 1)
 
 
 def step_kernel(
@@ -31,11 +36,13 @@
     free_hbm,
     loss_ref,
     grads_ref,
-    refreshed_ref,
+    refreshed_hbm,
     labels,
     features,
     weight,
     free,
+    fresh_rows,
+    id_counts,
     q_slots,
     q_rows,
     out_rows,
@@ -50,6 +57,9 @@
     load_sem,
     q_send,
     q_recv,
+    relay_send,
+    relay_recv,
+    fresh_sem,
     row_send,
     row_recv,
     half_send,
@@ -119,11 +129,19 @@
     loads[1].wait()
     hidden = jnp.dot(ordered, weight[...], preferred_element_type=f32)
     scale = lax.rsqrt(jnp.mean(hidden * hidden, axis=1, keepdims=True) + 1e-06)
-    encoded = hidden * scale * gain_ref[...]
+    encoded = hidden * scale * gain_ref[...].reshape(1, width)
     for c in range(n_cls):
         out_rows[c] = encoded[c * padded : (c + 1) * padded].astype(bf16)
 
     pl.semaphore_wait(barrier, total - 1)
+
+    partner = 1 - rep
+
+    def far(k):
+        return lax.rem(cls + 1 + lax.rem(k + n_cls // 2 - 2, n_cls - 1), n_cls)
+
+    def far_from(k):
+        return lax.rem(cls + n_cls - 1 - lax.rem(k + n_cls // 2 - 2, n_cls - 1), n_cls)
 
     def query_copy(other, slot):
         return pltpu.make_async_remote_copy(
@@ -131,7 +149,7 @@
             dst_ref=q_slots.at[slot],
             send_sem=q_send.at[other],
             recv_sem=q_recv.at[slot],
-            device_id=(other // n_rep, lax.rem(other, n_rep)),
+            device_id=(other, rep),
         )
 
     def row_copy(other, slot):
@@ -153,17 +171,33 @@
         )
 
     def send_query(k, carry):
-        query_copy(lax.rem(me + k, total), mine).start()
-        return carry
-
-    lax.fori_loop(1, total, send_query, 0)
+        query_copy(far(k), mine).start()
+        return carry
+
+    lax.fori_loop(1, n_cls, send_query, 0)
 
     def send_rows(k, carry):
-        row_copy(lax.rem(cls + k, n_cls), cls).start()
+        row_copy(far(k), cls).start()
         return carry
 
     lax.fori_loop(1, n_cls, send_rows, 0)
     in_rows[cls] = out_rows[cls]
+
+    def get_query(k, carry):
+        other = far_from(k)
+        query_copy(other, slot_of(other, rep)).wait_recv()
+        return carry
+
+    lax.fori_loop(1, n_cls, get_query, 0)
+    side = q_slots.at[pl.ds(rep * n_cls, n_cls)]
+    relay = pltpu.make_async_remote_copy(
+        src_ref=side,
+        dst_ref=side,
+        send_sem=relay_send,
+        recv_sem=relay_recv,
+        device_id=(cls, partner),
+    )
+    relay.start()
 
     my_base = (cls * slot_rows + rep * half_rows).astype(f32)
     wanted = my_base + row_i.astype(f32)
@@ -180,26 +214,28 @@
     seat_i = lax.broadcasted_iota(jnp.int32, (half_rows, n_cls * padded), 1)
     seating = jnp.where(seat_i == seat.astype(jnp.int32), 1.0, 0.0).astype(bf16)
 
-    def get_query(k, carry):
-        other = lax.rem(me + k, total)
-        slot = slot_of(other // n_rep, lax.rem(other, n_rep))
-        query_copy(other, slot).wait_recv()
-        return carry
-
-    lax.fori_loop(1, total, get_query, 0)
+    relay.wait_recv()
     for s in range(total):
         q_rows[s * query_rows : (s + 1) * query_rows] = q_slots[s].astype(f32)
     q = q_rows[...].astype(bf16)
 
-    ids = positives_ref[...]
+    n_pos = positives_ref.shape[1]
+    eye = eye_of(own_half)
+    ids = []
+    for p in range(n_pos):
+        rows = [positives_ref[r, p : p + 1, :].astype(f32) for r in range(n_rep)]
+        ids.append(jnp.concatenate([to_column(row, eye) for row in rows], axis=0).astype(jnp.int32))
+    valid = jnp.zeros((n_query, 1), f32)
+    for p in range(n_pos):
+        valid = valid + jnp.where(ids[p] >= 0, 1.0, 0.0)
+    id_counts[...] = jnp.broadcast_to(valid, id_counts.shape)
     slot_start = slot_ref[0] * slot_rows
-    n_pos = ids.shape[1]
 
     def counts_of(first, cols):
         label = first + lax.broadcasted_iota(jnp.int32, (n_query, cols), 1)
         count = jnp.zeros((n_query, cols), f32)
         for p in range(n_pos):
-            count = count + jnp.where(ids[:, p : p + 1] == label, 1.0, 0.0)
+            count = count + jnp.where(ids[p] == label, 1.0, 0.0)
         return count
 
     def weighted(block, peak, count, vectors):
@@ -239,18 +275,23 @@
 
     fresh_count = counts_of(cls * lab_rows + slot_start + rep * half_rows, half_rows)
 
+    def stage(c):
+        staged[pl.ds(pl.multiple_of(c * padded, 8), padded)] = in_rows[c].astype(f32)
+
     def get_rows(k, carry):
-        other = lax.rem(cls + n_cls - k, n_cls)
+        other = far_from(k)
         row_copy(other, other).wait_recv()
-        return carry
-
+        stage(other)
+        return carry
+
+    stage(cls)
     lax.fori_loop(1, n_cls, get_rows, 0)
-    for c in range(n_cls):
-        staged[c * padded : (c + 1) * padded] = in_rows[c].astype(f32)
     placed = jnp.dot(seating, staged[...].astype(bf16), preferred_element_type=f32)
     loads[2].wait()
-    refreshed_ref[...] = (free[...].astype(f32) + placed).astype(bf16)
-    vectors = refreshed_ref[...]
+    fresh_rows[...] = (free[...].astype(f32) + placed).astype(bf16)
+    vectors = fresh_rows[...]
+    store = pltpu.make_async_copy(fresh_rows, refreshed_hbm, fresh_sem)
+    store.start()
     block = lax.dot_general(q, vectors, NT, preferred_element_type=f32)
     fresh_peak = jnp.max(block, axis=1, keepdims=True)
     g, t, e, s = weighted(block, fresh_peak, fresh_count, vectors)
@@ -266,7 +307,6 @@
         half_out[r, :, 0:width] = grad[at]
         half_out[r, :, width : 2 * width] = hits[at]
         half_out[r, :, 2 * width :] = stats[at]
-    partner = 1 - rep
     swap = pltpu.make_async_remote_copy(
         src_ref=half_out.at[partner],
         dst_ref=half_in,
@@ -300,17 +340,16 @@
         shares_out[c, :, 2 * width :] = stats[at]
 
     def send_share(k, carry):
-        share_copy(lax.rem(cls + k, n_cls), cls).start()
+        share_copy(far(k), cls).start()
         return carry
 
     lax.fori_loop(1, n_cls, send_share, 0)
     shares_in[cls] = shares_out[cls]
 
-    own_ids = positives_ref[pl.ds(mine * query_rows, query_rows), :]
-    id_count = jnp.sum(jnp.where(own_ids >= 0, 1.0, 0.0), axis=1, keepdims=True)
+    id_count = id_counts[pl.ds(mine * query_rows, query_rows), :][:, 0:1]
 
     def get_share(k, carry):
-        other = lax.rem(cls + n_cls - k, n_cls)
+        other = far_from(k)
         share_copy(other, other).wait_recv()
         return carry
 
@@ -336,23 +375,26 @@
     wide = jnp.zeros((query_rows, width), f32)
     grad, hits, exp_sum, pos_sum = lax.fori_loop(0, n_cls, add, (wide, wide, zero, zero))
     loss = m + jnp.log(exp_sum) - pos_sum / id_count
-    loss_ref[...] = jnp.broadcast_to(loss, loss_ref.shape)
+    loss_ref[...] = jnp.sum(jnp.where(eye_of(query_rows), loss, 0.0), axis=0, keepdims=True)
     grads_ref[0] = (grad / exp_sum - hits / id_count).astype(bf16)
-
-    def end_query(k, carry):
-        query_copy(lax.rem(me + k, total), mine).wait_send()
-        return carry
-
-    lax.fori_loop(1, total, end_query, 0)
 
     def end_rows(k, carry):
         other = lax.rem(cls + k, n_cls)
+        query_copy(other, mine).wait_send()
         row_copy(other, cls).wait_send()
         share_copy(other, cls).wait_send()
         return carry
 
     lax.fori_loop(1, n_cls, end_rows, 0)
     swap.wait_send()
+    relay.wait_send()
+    store.wait()
+
+
+def pass_on(*refs):
+    half = len(refs) // 2
+    for source, target in zip(refs[:half], refs[half:]):
+        target[...] = source[...]
 
 
 def per_device(
@@ -383,20 +425,23 @@
     smem = pl.BlockSpec(memory_space=pltpu.SMEM)
     hbm = pl.BlockSpec(memory_space=pl.ANY)
     dma = pltpu.SemaphoreType.DMA
-    loss, grads, refreshed = pl.pallas_call(
+    outs = (
+        jax.ShapeDtypeStruct((1, query_rows), f32),
+        jax.ShapeDtypeStruct((1, query_rows, width), bf16),
+        jax.ShapeDtypeStruct((half_rows, width), bf16),
+    )
+    results = pl.pallas_call(
         functools.partial(step_kernel, n_cls, n_rep),
-        out_shape=(
-            jax.ShapeDtypeStruct((query_rows, 128), f32),
-            jax.ShapeDtypeStruct((1, query_rows, width), bf16),
-            jax.ShapeDtypeStruct((half_rows, width), bf16),
-        ),
+        out_shape=outs,
         in_specs=[smem, vmem, vmem, vmem, vmem, hbm, hbm, hbm, hbm],
-        out_specs=(vmem, vmem, vmem),
+        out_specs=(vmem, vmem, hbm),
         scratch_shapes=[
             pltpu.VMEM((usable, width), bf16),
             pltpu.VMEM((half_rows, width), bf16),
             pltpu.VMEM((width, width), bf16),
             pltpu.VMEM((half_rows, width), bf16),
+            pltpu.VMEM((half_rows, width), bf16),
+            pltpu.VMEM((n_query, STATS), f32),
             pltpu.VMEM((total, query_rows, width), bf16),
             pltpu.VMEM((n_query, width), f32),
             pltpu.VMEM((n_cls, padded, width), bf16),
@@ -409,8 +454,11 @@
             pltpu.VMEM((n_cls, query_rows, share), f32),
             pltpu.VMEM((n_cls, query_rows, share), f32),
             dma((3 + usable // slot_rows,)),
+            dma((n_cls,)),
             dma((total,)),
-            dma((total,)),
+            dma,
+            dma,
+            dma,
             dma((n_cls,)),
             dma((n_cls,)),
             dma,
@@ -424,15 +472,20 @@
     )(
         refresh_slot.reshape(1),
         queries,
-        positives.reshape(n_query, positives.shape[2]),
+        positives.transpose(0, 2, 1),
         targets.reshape(total, 1, half_rows),
-        encoder_gain.reshape(1, width),
+        encoder_gain,
         label_vectors,
         features,
         encoder_weight,
         free_vectors,
     )
-    return loss[:, 0].reshape(1, query_rows), grads, refreshed
+    return pl.pallas_call(
+        pass_on,
+        out_shape=outs,
+        in_specs=[vmem] * 3,
+        out_specs=(vmem,) * 3,
+    )(*results)
 
 
 def solution(mesh):

time: 44.7 us -> 39.4 us (0.88)
  local copies, waits for them, and re-layouts: 7.13 us -> 0 us
  Pallas kernels: 36 us -> 37.9 us
    unnamed x3 -> x0, local copies, waits for them, and re-layouts: 4.57 us -> none
    pallas_call x1 -> x2, Pallas kernels: 36 us -> 37.9 us  [the longest x1 35.9 us: per_device(): pl.pallas_call(functools.partial(step_kernel, n_cls, n_rep), out_shape=ou...]
    slice x1 -> x0, local copies, waits for them, and re-layouts: 1.29 us -> none  [per_device(): return (loss[:, 0].reshape(1, query_rows), grads, refreshed)]
    reshape x1 -> x0, local copies, waits for them, and re-layouts: 1.27 us -> none  [per_device(): encoder_gain.reshape(1, width)]
where the time goes in v2:
time: 39.4 us; the launch traced here: 39.2 us
  Pallas kernels  37.9 us (96%)
  between operations  1.29 us (3%)
    pallas_call x1, Pallas kernels, per_device(): pl.pallas_call(functools.partial(step_kernel, n_cls, n_rep), out_shape=ou...  35.9 us
    pallas_call x1, Pallas kernels, per_device(): pl.pallas_call(pass_on, out_shape=outs, in_specs=[vmem] * 3, out_specs=(v...  1.93 us

profile of v2, /device:TPU:1, one launch (start us, length us, event | category | flops | bytes accessed | tf_op | source)
XLA Modules:
  0.0 39.2 jit_solution(4133350526121562487)
XLA Ops:
  1.3 35.9 %shard_map.112 = (f32[1,2]{1,0:T(1,128)}, bf16[1,2,768]{2,1,0:T(2,128)(2,1)}, bf16[384,768]{1,0:T(8,128)(2,1)}) custom-call(s32[1]{0:T(128)} %bitcast.3.slot_ref, bf16[1,2,768]{2,1,0:T(2,128)(2,1)} %queries_ref.1, s32[2,4,32]{2,1,0:T(4,128)} %bitcast.5, s32[32,1,384]{2,1,0:T(1,128)} %bitcast.4, f32[768]{0:T(1024)} %gain_ref.1, bf16[6144,768]{1,0:T(8,128)(2,1)} %labels_hbm.1, ...), custom_call_target="tpu_custom_call" | custom-call | tf_op jit(solution)/shard_map/pallas_call | solution.py:433
  37.2 1.9 %shard_map.113 = (f32[1,2]{1,0:T(1,128)}, bf16[1,2,768]{2,1,0:T(2,128)(2,1)}, bf16[384,768]{1,0:T(8,128)(2,1)}) custom-call(f32[1,2]{1,0:T(1,128)} %get-tuple-element.6.refs_0_, bf16[1,2,768]{2,1,0:T(2,128)(2,1)} %get-tuple-element.7.refs_1_, bf16[384,768]{1,0:T(8,128)(2,1)} %get-tuple-element.8.refs_2_), custom_call_target="tpu_custom_call" | custom-call | tf_op jit(solution)/shard_map/pallas_call | solution.py:483
